TPU v7x, 256 devices: a whole 4x4x8 slice. The times are simulated.
256 devices in a mesh: dp: 32 (over x, z), seq: 8 (over y, core).
Axes of the slice: x: 4, y: 4, z: 8, core: 2. Of those that a mesh axis runs over, the one named last changes fastest.
Arguments:
- hidden: bfloat16 [32, 8192, 4096], P('dp', 'seq'), may hold values from -6 to 6
- value_weight: bfloat16 [4096, 64], replicated, may hold values from -0.09375 to 0.09375
- value_bias: float32 [64], replicated, may hold values from -1 to 1
- returns: float32 [32, 8192], P('dp', 'seq'), may hold values from -12 to 12, as said below
- task_bins: int32 [32, 8192], P('dp', 'seq'), may hold values from 0 to 63
- loss_mask: int32 [32, 8192], P('dp', 'seq'), may hold values 0 or 1
Outputs:
- targets: float32 [32, 8192], P('dp', 'seq')
- weight_grad: float32 [4096, 64], replicated
- bias_grad: float32 [64], replicated
Inputs may be any that keep to these rules, and one draw needn't show every extreme that they name: The returns of one rollout share a level and a trend along positions.
All inputs are finite; a program needn't handle non-finite values.
Results may differ from a plain program's by a relative error of at most 0.00083.
Values sent between devices are 32-bit elements.
A program may use at most 64 MiB of HBM per device.

v0:
```python
import jax
import jax.numpy as jnp
from jax import lax
from jax.sharding import Mesh
from jax.sharding import PartitionSpec as P

DP = ("dp_0", "dp_1")
DP_SEQ = ("dp_0", "dp_1", "seq_0", "seq_1")
SEQ = ("seq_0", "seq_1")


def one_axis_at_a_time(x, axes):
    for axis in axes:
        x = lax.psum(x, axis)
    return x


def in_blocks(x, dim, devices):
    shape = x.shape
    pieces = x.reshape(*shape[:dim], devices, shape[dim] // devices, *shape[dim + 1 :])
    return jnp.moveaxis(pieces, dim, 0)


def sent_and_summed(x, axis, dim):
    devices = lax.axis_size(axis)
    pieces = lax.all_to_all(in_blocks(x, dim, devices), axis, 0, 0, tiled=True)
    return jnp.sum(pieces, axis=0)


def over_pieces(x, axis):
    pieces = lax.all_gather(x, axis)
    return pieces.sum(axis=0)


def in_order(pieces, dim):
    pieces = jnp.moveaxis(pieces, 0, dim)
    shape = pieces.shape
    return pieces.reshape(*shape[:dim], shape[dim] * shape[dim + 1], *shape[dim + 2 :])


def one_gather(arrays, axis, dims):
    ravelled = jnp.concatenate([a.reshape(-1) for a in arrays])
    lines, at, outs = (lax.all_gather(ravelled, axis), 0, [])
    for a, dim in zip(arrays, dims):
        pieces = lines[:, at : at + a.size].reshape(-1, *a.shape)
        outs.append(in_order(pieces, dim))
        at += a.size
    return tuple(outs)


def on_device(hidden, value_weight, value_bias, returns, task_bins, loss_mask):
    rollouts = hidden.shape[0] * lax.axis_size(DP)
    states = hidden.reshape(-1, hidden.shape[2])
    flat_returns = returns.reshape(-1)
    bins_iota = jnp.arange(value_weight.shape[1], dtype=jnp.int32)
    chosen = (task_bins.reshape(-1)[:, None] == bins_iota).astype(jnp.float32)
    valid = loss_mask.reshape(-1).astype(jnp.float32)
    onehot = chosen * valid[:, None]
    scores = jnp.dot(states, value_weight, preferred_element_type=jnp.float32)
    counts = jnp.sum(onehot, axis=0)
    summed = jnp.sum(onehot * flat_returns[:, None], axis=0)
    squares = jnp.sum(onehot * flat_returns[:, None] * flat_returns[:, None], axis=0)
    counts, summed, squares = (
        one_axis_at_a_time(counts, DP_SEQ),
        one_axis_at_a_time(summed, DP_SEQ),
        one_axis_at_a_time(squares, DP_SEQ),
    )
    means = summed / jnp.maximum(counts, 1.0)
    second = squares - summed * means
    floor_counts = jnp.maximum(counts, 1.0)
    spread = jnp.sqrt(second / floor_counts + 0.1)
    deviation = flat_returns[:, None] - means
    targets = jnp.sum(chosen * (deviation / spread), axis=-1)
    predicted = jnp.sum((scores + value_bias) * chosen, axis=-1)
    slope = valid * jnp.clip(predicted - targets, -1.0, 1.0) / rollouts
    coefficient = chosen * slope[:, None]
    weight_grad = lax.dot_general(
        states,
        coefficient.astype(jnp.bfloat16),
        (((0,), (0,)), ((), ())),
        preferred_element_type=jnp.float32,
    )
    bias_grad = jnp.sum(coefficient, axis=0)
    weight_share, bias_share = (
        sent_and_summed(weight_grad, SEQ, 0),
        sent_and_summed(bias_grad, SEQ, 0),
    )
    weight_share, bias_share = (over_pieces(weight_share, DP), over_pieces(bias_share, DP))
    weight_grad, bias_grad = one_gather((weight_share, bias_share), SEQ, (0, 0))
    return (targets.reshape(returns.shape), weight_grad, bias_grad)


def solution(mesh):
    torus = Mesh(mesh.devices.reshape(4, 8, 4, 2), ("dp_0", "dp_1", "seq_0", "seq_1"))
    return jax.shard_map(
        on_device,
        mesh=torus,
        in_specs=(P(DP, SEQ, None), P(), P(), P(DP, SEQ), P(DP, SEQ), P(DP, SEQ)),
        out_specs=(P(DP, SEQ), P(), P()),
        check_vma=False,
    )
```

profile of v0, /device:TPU:1, one launch (start us, length us, event | category | flops | bytes accessed | tf_op | source)
XLA Modules:
  0.0 241.2 jit_solution(15174251492240911007)
XLA Ops:
  7.2 0.0 copy-start
  7.2 0.0 all-gather.5.cloned.1.call-start
  7.2 0.7 convert_element_type.17
  8.0 0.9 fusion.14
  8.9 9.3 %all-reduce.4 = (f32[64]{0:T(128)S(1)}, f32[64]{0:T(128)S(1)}, f32[64]{0:T(128)S(1)}) all-reduce(f32[64]{0:T(128)S(1)} %get-tuple-element.13, f32[64]{0:T(128)S(1)} %get-tuple-element.12, f32[64]{0:T(128)S(1)} %get-tuple-element.14), channel_id=1, replica_groups=mesh['dp_0'=4,'dp_1'=8,'seq_0'=4,'seq_1'=2] {'dp_0'}, use_global_device_ids=true, to_apply=%region_11.0 | all-reduce | flops 192 | bytes 1536 | tf_op jit(solution)/shard_map/psum | solution.py:14
  18.2 16.2 %all-reduce.2 = (f32[64]{0:T(128)S(1)}, f32[64]{0:T(128)S(1)}, f32[64]{0:T(128)S(1)}) all-reduce(f32[64]{0:T(128)S(1)} %get-tuple-element.21, f32[64]{0:T(128)S(1)} %get-tuple-element.22, f32[64]{0:T(128)S(1)} %get-tuple-element.23), channel_id=1, replica_groups=mesh['dp_0'=4,'dp_1'=8,'seq_0'=4,'seq_1'=2] {'dp_1'}, use_global_device_ids=true, to_apply=%region_12.0 | all-reduce | flops 192 | bytes 1536 | tf_op jit(solution)/shard_map/psum | solution.py:14
  34.4 8.7 %all-reduce.3 = (f32[64]{0:T(128)S(1)}, f32[64]{0:T(128)S(1)}, f32[64]{0:T(128)S(1)}) all-reduce(f32[64]{0:T(128)S(1)} %get-tuple-element.15, f32[64]{0:T(128)S(1)} %get-tuple-element.16, f32[64]{0:T(128)S(1)} %get-tuple-element.17), channel_id=1, replica_groups=mesh['dp_0'=4,'dp_1'=8,'seq_0'=4,'seq_1'=2] {'seq_0'}, use_global_device_ids=true, to_apply=%region_13.0 | all-reduce | flops 192 | bytes 1536 | tf_op jit(solution)/shard_map/psum | solution.py:14
  43.1 10.6 %all-reduce.5 = (f32[64]{0:T(128)S(1)}, f32[64]{0:T(128)S(1)}, f32[64]{0:T(128)S(1)}) all-reduce(f32[64]{0:T(128)S(1)} %get-tuple-element.18, f32[64]{0:T(128)S(1)} %get-tuple-element.19, f32[64]{0:T(128)S(1)} %get-tuple-element.20), channel_id=1, replica_groups=mesh['dp_0'=4,'dp_1'=8,'seq_0'=4,'seq_1'=2] {'seq_1'}, use_global_device_ids=true, to_apply=%region_14.0 | all-reduce | flops 192 | bytes 1536 | tf_op jit(solution)/shard_map/psum | solution.py:14
  53.7 0.8 select_reduce_fusion.2
  54.6 0.0 copy-done
  54.6 0.0 copy-start.4
  54.6 0.0 copy-start.1
  54.6 0.0 copy-start.3
  54.6 6.2 %fusion.10 = f32[1024]{0:T(1024)S(1)} fusion(bf16[4096,64]{0,1:T(8,128)(2,1)S(1)} %copy-done, bf16[1,1024,4096]{2,1,0:T(8,128)(2,1)} %param.6, f32[64]{0:T(128)} %param.8, s32[1024]{0:T(1024)} %bitcast.34), kind=kOutput, calls=%fused_computation.7 | convolution fusion | flops 537132032 | bytes 8921344 | tf_op jit(solution)/shard_map/dot_general | solution.py:59
  60.8 0.0 copy-done.4
  60.9 0.0 copy-done.1
  60.9 0.0 copy-done.3
  60.9 1.6 fusion
  62.5 0.0 copy-start.6
  62.5 0.0 copy-start.5
  62.5 0.1 copy.23
  62.6 17.7 %all_to_all.14 = f32[8,512,64]{1,2,0:T(8,128)S(1)} all-to-all(f32[8,512,64]{1,2,0:T(8,128)S(1)} %bitcast.30), channel_id=1, replica_groups=mesh['dp_0'=4,'dp_1'=8,'seq_0'=4,'seq_1'=2] {'seq_0','seq_1'}, dimensions={0} | all-to-all | bytes 2097152 | tf_op jit(solution)/shard_map/all_to_all | solution.py:26
  80.3 0.7 reduce_sum.95
  81.0 0.0 all-gather.5.cloned.1.call-update
  81.0 0.1 select_reduce_fusion
  81.1 0.7 all_to_all.10
  81.8 4.2 %all-to-all-start.1 = ((f32[8,1,8]{2,1,0:T(1,128)}), f32[8,1,8]{2,1,0:T(1,128)S(1)}, u32[]{:S(2)}, u32[]{:S(2)}) async-start(f32[8,1,8]{2,1,0:T(1,128)} %bitcast.6), calls=%async_computation.1 | async-start | bytes 8192 | tf_op jit(solution)/shard_map/all_to_all | solution.py:26
  86.0 0.6 dynamic-slice.1
  86.6 0.6 dynamic-slice
  88.5 2.1 all-to-all-done.1
  90.7 0.2 dynamic-update-slice
  90.9 56.0 %all-reduce = f32[256]{0:T(256)S(1)} all-reduce(f32[256]{0:T(256)S(1)} %dynamic-update-slice), channel_id=3, replica_groups=mesh['dp_0'=4,'dp_1'=8,'seq_0'=4,'seq_1'=2] {'dp_0','dp_1'}, use_global_device_ids=true, to_apply=%add | all-reduce | flops 256 | bytes 2048
  146.9 0.1 reshape.54
  147.0 6.8 %all-gather.5.cloned.1.call-done = f32[16384,64]{0,1:T(8,128)} async-done(((f32[512,64]{0,1:T(8,128)}), f32[16384,64]{0,1:T(8,128)}) %all-gather.5.cloned.1.call-update) | async-done | bytes 4194320 | tf_op jit(solution)/shard_map/all_gather | solution.py:31
  153.8 4.6 %copy.21 = f32[8,8,32,512]{3,2,1,0:T(8,128)S(1)} copy(f32[8,8,32,512]{3,1,2,0:T(8,128)} %bitcast.29) | data formatting | bytes 8388608
  158.3 0.7 bitcast_reduce_fusion
  159.0 0.1 copy.16
  159.1 0.1 reshape.51
  159.2 0.1 broadcast.28
  159.3 0.5 maximum_dynamic-update-slice_fusion
  159.8 1.0 copy-done.2
  160.9 0.0 all-reduce.8.cloned.1.call-update
  160.9 66.4 %all-reduce.8.cloned.1.call-done = f32[262208]{0:T(1024)} async-done(((f32[262208]{0:T(1024)}), f32[262208]{0:T(1024)}) %all-reduce.8.cloned.1.call-update) | async-done | bytes 1048848
  227.3 1.8 reshape.55
  229.1 1.0 slice.8
  230.2 0.6 reshape.52
  230.7 2.1 reshape_reshape.3
  232.8 1.6 copy.18
  (10 shorter events, 0.1 us)
Async XLA Ops:
  7.2 47.4 %copy-start = (bf16[4096,64]{0,1:T(8,128)(2,1)S(1)}, bf16[4096,64]{0,1:T(8,128)(2,1)}, u32[]{:S(2)}) copy-start(bf16[4096,64]{0,1:T(8,128)(2,1)} %param.7) | copy-start | bytes 1572868
  7.2 146.6 %all-gather.5.cloned.1.call-start = ((), (), s32[]{:S(2)}) async-start(), calls=%async_computation.2 | async-start | bytes 4325376 | tf_op jit(solution)/shard_map/all_gather | solution.py:31
  54.6 6.3 %copy-start.4 = (f32[1024]{0:T(1024)}, f32[1024]{0:T(1024)S(1)}, u32[]{:S(2)}) copy-start(f32[1024]{0:T(1024)S(1)} %select_reduce_fusion.2) | copy-start | bytes 12292
  54.6 6.3 %copy-start.1 = (bf16[1,1024,4096]{2,1,0:T(8,128)(2,1)S(1)}, bf16[1,1024,4096]{2,1,0:T(8,128)(2,1)}, u32[]{:S(2)}) copy-start(bf16[1,1024,4096]{2,1,0:T(8,128)(2,1)} %param.6) | copy-start | bytes 25165828
  54.6 6.3 %copy-start.3 = (s32[1,1024]{1,0:T(1,128)S(1)}, s32[1,1024]{1,0:T(1,128)}, u32[]{:S(2)}) copy-start(s32[1,1024]{1,0:T(1,128)} %param.10) | copy-start | bytes 12292
  62.5 23.6 %copy-start.6 = (u32[256]{0:T(256)S(1)}, u32[256]{0:T(256)}, u32[]{:S(2)}) copy-start(u32[256]{0:T(256)} %constant.27) | copy-start | bytes 3076
  62.5 24.2 %copy-start.5 = (u32[256]{0:T(256)S(1)}, u32[256]{0:T(256)}, u32[]{:S(2)}) copy-start(u32[256]{0:T(256)} %constant.22) | copy-start | bytes 3076
  81.8 8.8 %all-to-all-start.1 = ((f32[8,1,8]{2,1,0:T(1,128)}), f32[8,1,8]{2,1,0:T(1,128)S(1)}, u32[]{:S(2)}, u32[]{:S(2)}) async-start(f32[8,1,8]{2,1,0:T(1,128)} %bitcast.6), calls=%async_computation.1 | async-start | bytes 8192 | tf_op jit(solution)/shard_map/all_to_all | solution.py:26
  86.0 141.3 %all-reduce.8.cloned.1.call-start = ((), (), s32[]{:S(2)}) async-start(), calls=%async_computation.3 | async-start | bytes 2105344
  159.8 1.0 copy-start.2
Sparse Core Ops, SparseCore 0:
  81.1 72.5 all-gather.4
  161.0 66.2 all-reduce.7
where the time goes:
time: 243 us; the launch traced here: 241 us
  blocking collectives  118 us (49%)
  waiting for transfers between devices  75.4 us (31%)
  between operations  15.5 us (6%)
  local copies, waits for them, and re-layouts  15.2 us (6%)
  matrix products  7.79 us (3%)
  other arithmetic  4.6 us (2%)
  starting transfers between devices  4.24 us (2%)
    unnamed x3, waiting for transfers between devices  66.4 us
    unnamed x1, blocking collectives  56 us
    psum x4, blocking collectives, one_axis_at_a_time(): x = lax.psum(x, axis)  44.8 us
    all_to_all x1, blocking collectives, sent_and_summed(): pieces = lax.all_to_all(in_blocks(x, dim, devices), axis, 0, 0, tiled=True)  17.7 us
    unnamed x21, local copies, waits for them, and re-layouts  8.7 us
    all_gather x1, waiting for transfers between devices, over_pieces(): pieces = lax.all_gather(x, axis)  6.77 us
    dot_general x1, matrix products, on_device(): scores = jnp.dot(states, value_weight, preferred_element_type=jnp.float32)  6.22 us
  transfers between devices with their start and end apart: 3, of which 3 were waited for; matrix products, arithmetic and copies ran while one was open for 1% of the time, Pallas kernels for 0%

commit v1 on v0

v1 whole, which is shorter than its diff:
```python
import functools

import jax
import jax.numpy as jnp
from jax import lax
from jax.experimental import pallas as pl
from jax.experimental.pallas import tpu as pltpu
from jax.sharding import Mesh
from jax.sharding import PartitionSpec as P

NX, NZ, NY, NC = 4, 8, 4, 2
MESH = pl.DeviceIdType.MESH
HIGHEST = lax.Precision.HIGHEST
TOKENS, D, NB = 1024, 4096, 64
PIECES = 4
ROWS = TOKENS // PIECES
BLOCK = 512
HALF = D // 2
LAG = 3
ORDER = ((0, 2), (1, 2), (0, 1), (1, 1), (0, 3), (1, 3), (0, 0), (1, 0))


def dot(a, b, dims, precision=None):
    return lax.dot_general(a, b, (dims, ((), ())), precision=precision, preferred_element_type=jnp.float32)


def kernel(
    rollouts,
    hidden_hbm, weight_hbm, bias_hbm, returns_hbm, bins_hbm, mask_hbm,
    targets_ref, grad_ref, bias_grad_ref,
    hidden, weight, bias, returns, bins, mask,
    predicted, coefficient,
    stats_line, stats_plane, bias_line, bias_plane,
    parts, from_core, summed, got_first, kept, got_second, tiles, got_third,
    hidden_sem, in_sem, small_send, small_recv,
    core_send, core_recv, first_send, first_recv, second_send, second_recv, third_send, third_recv,
    back_third_send, back_third_recv, back_second_send, back_second_recv,
    back_first_send, back_first_recv, back_core_send, back_core_recv,
):
    x, z, y, c = (lax.axis_index(name) for name in ("x", "z", "y", "c"))

    def at(x=x, z=z, y=y, c=c):
        return {"x": x, "z": z, "y": y, "c": c}

    loads = [
        pltpu.make_async_copy(src, dst, in_sem.at[i])
        for i, (src, dst) in enumerate(
            ((returns_hbm, returns), (bins_hbm, bins), (mask_hbm, mask), (bias_hbm, bias), (weight_hbm, weight))
        )
    ]
    for load in loads:
        load.start()
    pieces = [
        pltpu.make_async_copy(
            hidden_hbm.at[0, pl.ds(i * ROWS, ROWS)], hidden.at[pl.ds(i * ROWS, ROWS)], hidden_sem.at[i]
        )
        for i in range(PIECES)
    ]
    for piece in pieces:
        piece.start()

    barrier = pltpu.get_barrier_semaphore()

    def in_line(k):
        return at(z=lax.rem(z + k // 2, NZ), c=lax.rem(c + k, NC))

    def in_plane(k):
        return at(x=lax.rem(x + k // NY, NX), y=lax.rem(y + k, NY))

    def greet(k, carry):
        pl.semaphore_signal(barrier, inc=1, device_id=in_line(k), device_id_type=MESH)
        pl.semaphore_signal(barrier, inc=1, device_id=in_plane(k), device_id_type=MESH)
        return carry

    lax.fori_loop(1, 16, greet, 0)

    def send_all(buffer, slot, sem, peer):
        def body(k, carry):
            pltpu.make_async_remote_copy(
                src_ref=buffer.at[slot],
                dst_ref=buffer.at[slot],
                send_sem=small_send.at[sem],
                recv_sem=small_recv.at[sem],
                device_id=peer(k),
                device_id_type=MESH,
            ).start()
            return carry

        lax.fori_loop(1, 16, body, 0)

    def wait_all(buffer, sems, sem):
        fifteen = buffer.at[pl.ds(0, 15)]
        pltpu.make_async_copy(fifteen, fifteen, sems.at[sem]).wait()

    my_line = z * NC + c
    my_plane = x * NY + y

    for load in loads[:3]:
        load.wait()
    ret = returns[...]
    ids = bins[...]
    valid = mask[...].astype(jnp.float32)
    chosen = (lax.broadcasted_iota(jnp.int32, (NB, TOKENS), 0) == ids).astype(jnp.float32)
    row = lax.broadcasted_iota(jnp.int32, (8, TOKENS), 0)
    moments = jnp.where(row == 0, valid, jnp.where(row == 1, valid * ret, jnp.where(row == 2, valid * ret * ret, 0.0)))
    local = dot(moments, chosen, ((1,), (1,)), HIGHEST)
    padding = jnp.zeros((8, 128 - NB), jnp.float32)
    stats_line[my_line] = jnp.concatenate([local, padding], axis=1)

    pl.semaphore_wait(barrier, 30)
    send_all(stats_line, my_line, 0, in_line)

    loads[4].wait()
    for i in range(PIECES):
        pieces[i].wait()
        scores = dot(weight[...], hidden[pl.ds(i * ROWS, ROWS), :], ((1,), (1,)))
        predicted[:, pl.ds(i * ROWS, ROWS)] = jnp.sum(
            jnp.where(lax.broadcasted_iota(jnp.int32, (NB, ROWS), 0) == bins[:, pl.ds(i * ROWS, ROWS)], scores, 0.0),
            axis=0,
            keepdims=True,
        )

    wait_all(stats_line, small_recv, 0)
    total = stats_line[0]
    for i in range(1, 16):
        total = total + stats_line[i]
    stats_plane[my_plane] = total
    send_all(stats_plane, my_plane, 1, in_plane)
    loads[3].wait()
    wait_all(stats_plane, small_recv, 1)
    total = stats_plane[0]
    for i in range(1, 16):
        total = total + stats_plane[i]

    counts = jnp.maximum(total[0:1, :NB], 1.0)
    means = total[1:2, :NB] / counts
    second = total[2:3, :NB] - total[1:2, :NB] * means
    spread = jnp.sqrt(second / counts + 0.1)
    table_row = lax.broadcasted_iota(jnp.int32, (8, NB), 0)
    table = jnp.where(
        table_row == 0, means, jnp.where(table_row == 1, spread, jnp.where(table_row == 2, bias[...], 0.0))
    )
    chosen = (lax.broadcasted_iota(jnp.int32, (NB, TOKENS), 0) == bins[...]).astype(jnp.float32)
    own = dot(table, chosen, ((1,), (0,)), HIGHEST)
    targets = (returns[...] - own[0:1]) / own[1:2]
    targets_ref[...] = targets
    slope = mask[...].astype(jnp.float32) * jnp.clip(predicted[...] + own[2:3] - targets, -1.0, 1.0) / rollouts
    coefficient[...] = (chosen * slope).astype(jnp.bfloat16)
    slopes = jnp.where(row == 0, slope, 0.0)
    local = dot(slopes, chosen, ((1,), (1,)), HIGHEST)
    bias_line[my_line] = jnp.concatenate([local, padding], axis=1)
    send_all(bias_line, my_line, 2, in_line)

    mine = pl.ds(pl.multiple_of(c * 32, 32), 32)
    others = pl.ds(pl.multiple_of((1 - c) * 32, 32), 32)
    sizes = (NX, NY)

    def first_peer(half, k):
        return at(x=lax.rem(x + k, NX)) if half == 0 else at(y=lax.rem(y + k, NY))

    def second_peer(half, k):
        return at(y=lax.rem(y + k, NY)) if half == 0 else at(x=lax.rem(x + k, NX))

    first_at, second_at = (x, y), (y, x)

    def copy(src, dst, send, recv, peer):
        return pltpu.make_async_remote_copy(
            src_ref=src, dst_ref=dst, send_sem=send, recv_sem=recv, device_id=peer, device_id_type=MESH
        )

    sent = []

    def core_copy(s):
        return copy(parts.at[s, others], from_core.at[s], core_send.at[s], core_recv.at[s], at(c=1 - c))

    def first_copy(s):
        half, k = ORDER[s]
        return copy(
            summed.at[s], got_first.at[half, k - 1], first_send.at[half, k - 1], first_recv.at[half, k - 1],
            first_peer(half, k),
        )

    def finish(s):
        core_copy(s).wait_recv()
        summed[s] = parts[s, mine] + from_core[s]
        if ORDER[s][1]:
            first_copy(s).start()

    for s, (half, k) in enumerate(ORDER):
        owner = lax.rem(first_at[half] + k, 4)
        columns = pl.ds(pl.multiple_of(half * HALF + owner * BLOCK, BLOCK), BLOCK)
        parts[s] = dot(coefficient[...], hidden[:, columns], ((1,), (0,)))
        core_copy(s).start()
        if s >= LAG:
            finish(s - LAG)
    for s in range(len(ORDER) - LAG, len(ORDER)):
        finish(s)

    wait_all(bias_line, small_recv, 2)
    total = bias_line[0]
    for i in range(1, 16):
        total = total + bias_line[i]
    bias_plane[my_plane] = total
    send_all(bias_plane, my_plane, 3, in_plane)

    def second_copy(half, k):
        there = lax.rem(second_at[half] + k, 4)
        return copy(
            kept.at[half, :, pl.ds(pl.multiple_of(there * 128, 128), 128)], got_second.at[half, k - 1],
            second_send.at[half, k - 1], second_recv.at[half, k - 1], second_peer(half, k),
        )

    for half in range(2):
        s = ORDER.index((half, 0))
        for k in (1, 3, 2):
            first_copy(ORDER.index((half, k))).wait_recv()
        kept[half] = summed[s] + got_first[half, 0] + got_first[half, 1] + got_first[half, 2]
        for k in (2, 1, 3):
            second_copy(half, k).start()

    def third_copy(k):
        there = lax.rem(z + k, NZ)
        return copy(tiles.at[there], got_third.at[k - 1], third_send.at[k - 1], third_recv.at[k - 1], at(z=there))

    for half in range(2):
        for k in (1, 3, 2):
            second_copy(half, k).wait_recv()
        here = pl.ds(pl.multiple_of(second_at[half] * 128, 128), 128)
        block = kept[half, :, here] + got_second[half, 0] + got_second[half, 1] + got_second[half, 2]
        for i in range(4):
            tiles[half * 4 + i] = block[i * 8 : i * 8 + 8]
    for k in (4, 3, 5, 2, 6, 1, 7):
        third_copy(k).start()
    for k in (1, 7, 2, 6, 3, 5, 4):
        third_copy(k).wait_recv()
    tile = tiles[z]
    for k in range(1, NZ):
        tile = tile + got_third[k - 1]

    column_of = (x * BLOCK + y * 128, HALF + y * BLOCK + x * 128)
    high = z // 4
    place = grad_ref.at[
        pl.ds(pl.multiple_of(c * 32 + (z - 4 * high) * 8, 8), 8),
        pl.ds(pl.multiple_of(column_of[0] + high * (column_of[1] - column_of[0]), 128), 128),
    ]
    place[...] = tile

    def back_third(k):
        return copy(place, place, back_third_send.at[k - 1], back_third_recv.at[k - 1], at(z=lax.rem(z + k, NZ)))

    def back_second(half, k):
        spot = grad_ref.at[mine, pl.ds(pl.multiple_of(column_of[half], 128), 128)]
        return copy(
            spot, spot, back_second_send.at[half, k - 1], back_second_recv.at[half, k - 1], second_peer(half, k)
        )

    def back_first(half, k):
        spot = grad_ref.at[mine, pl.ds(pl.multiple_of(half * HALF + first_at[half] * BLOCK, BLOCK), BLOCK)]
        return copy(spot, spot, back_first_send.at[half, k - 1], back_first_recv.at[half, k - 1], first_peer(half, k))

    def back_core(half, k):
        owner = lax.rem(first_at[half] + 4 - k, 4)
        spot = grad_ref.at[mine, pl.ds(pl.multiple_of(half * HALF + owner * BLOCK, BLOCK), BLOCK)]
        return copy(spot, spot, back_core_send.at[half, k], back_core_recv.at[half, k], at(c=1 - c))

    for k in (4, 3, 5, 2, 6, 1, 7):
        back_third(k).start()
    for k in (1, 7, 2, 6, 3, 5, 4):
        back_third(k).wait_recv()
    for half in range(2):
        for k in (2, 1, 3):
            back_second(half, k).start()
    for half in range(2):
        for k in (1, 3, 2):
            back_second(half, k).wait_recv()
        for k in (2, 1, 3):
            back_first(half, k).start()
        back_core(half, 0).start()

    wait_all(bias_plane, small_recv, 3)
    total = bias_plane[0]
    for i in range(1, 16):
        total = total + bias_plane[i]
    bias_grad_ref[...] = total[0:1, :NB]

    for k in (1, 3, 2):
        for half in range(2):
            back_first(half, k).wait_recv()
            back_core(half, k).start()
    for half in range(2):
        for k in range(4):
            back_core(half, k).wait_recv()

    for i, buffer in enumerate((stats_line, stats_plane, bias_line, bias_plane)):
        wait_all(buffer, small_send, i)
    for s, (half, k) in enumerate(ORDER):
        core_copy(s).wait_send()
        if k:
            first_copy(s).wait_send()
            second_copy(half, k).wait_send()
            back_second(half, k).wait_send()
            back_first(half, k).wait_send()
        back_core(half, k).wait_send()
    for k in range(1, NZ):
        third_copy(k).wait_send()
        back_third(k).wait_send()


def on_device(hidden, value_weight, value_bias, returns, task_bins, loss_mask):
    rollouts = hidden.shape[0] * lax.axis_size(("x", "z"))
    f32 = jnp.float32
    dma = pltpu.SemaphoreType.DMA
    any_space = pl.BlockSpec(memory_space=pl.ANY)
    vmem = pl.BlockSpec(memory_space=pltpu.VMEM)
    small = pltpu.VMEM((16, 8, 128), f32)
    targets, grad, bias_grad = pl.pallas_call(
        functools.partial(kernel, rollouts),
        out_shape=(
            jax.ShapeDtypeStruct((1, TOKENS), f32),
            jax.ShapeDtypeStruct((NB, D), f32),
            jax.ShapeDtypeStruct((1, NB), f32),
        ),
        in_specs=[any_space] * 6,
        out_specs=(vmem, vmem, vmem),
        scratch_shapes=[
            pltpu.VMEM((TOKENS, D), jnp.bfloat16),
            pltpu.VMEM((NB, D), jnp.bfloat16),
            pltpu.VMEM((1, NB), f32),
            pltpu.VMEM((1, TOKENS), f32),
            pltpu.VMEM((1, TOKENS), jnp.int32),
            pltpu.VMEM((1, TOKENS), jnp.int32),
            pltpu.VMEM((1, TOKENS), f32),
            pltpu.VMEM((NB, TOKENS), jnp.bfloat16),
            small, small, small, small,
            pltpu.VMEM((8, NB, BLOCK), f32),
            pltpu.VMEM((8, 32, BLOCK), f32),
            pltpu.VMEM((8, 32, BLOCK), f32),
            pltpu.VMEM((2, 3, 32, BLOCK), f32),
            pltpu.VMEM((2, 32, BLOCK), f32),
            pltpu.VMEM((2, 3, 32, 128), f32),
            pltpu.VMEM((8, 8, 128), f32),
            pltpu.VMEM((7, 8, 128), f32),
            dma((PIECES,)), dma((5,)), dma((4,)), dma((4,)),
            dma((8,)), dma((8,)), dma((2, 3)), dma((2, 3)), dma((2, 3)), dma((2, 3)), dma((7,)), dma((7,)),
            dma((7,)), dma((7,)), dma((2, 3)), dma((2, 3)), dma((2, 3)), dma((2, 3)), dma((2, 4)), dma((2, 4)),
        ],
        compiler_params=pltpu.CompilerParams(
            collective_id=0, has_side_effects=True, vmem_limit_bytes=60 * 1024 * 1024
        ),
    )(hidden, value_weight.T, value_bias.reshape(1, NB), returns, task_bins, loss_mask)
    return targets, grad.T, bias_grad.reshape(NB)


def solution(mesh):
    torus = Mesh(mesh.devices.reshape(NX, NZ, NY, NC), ("x", "z", "y", "c"))
    dp, seq = ("x", "z"), ("y", "c")
    return jax.shard_map(
        on_device,
        mesh=torus,
        in_specs=(P(dp, seq, None), P(), P(), P(dp, seq), P(dp, seq), P(dp, seq)),
        out_specs=(P(dp, seq), P(), P()),
        check_vma=False,
    )
```

time: 243 us -> 60.5 us (0.25)
  blocking collectives: 118 us -> 0 us
  waiting for transfers between devices: 75.4 us -> 0 us
  Pallas kernels: 0 us -> 55 us
  between operations: 15.5 us -> 0.64 us
  local copies, waits for them, and re-layouts: 15.2 us -> 4.68 us
  matrix products: 7.79 us -> 0 us
  other arithmetic: 4.6 us -> 0 us
  starting transfers between devices: 4.24 us -> 0 us
    unnamed x3 -> x0, waiting for transfers between devices: 66.4 us -> none
    unnamed x1 -> x0, blocking collectives: 56 us -> none
    pallas_call x0 -> x1, Pallas kernels: none -> 55 us  [on_device(): pl.pallas_call(functools.partial(kernel, rollouts), out_shape=(jax.ShapeD...]
    psum x4 -> x0, blocking collectives: 44.8 us -> none  [one_axis_at_a_time(): x = lax.psum(x, axis)]
    all_to_all x1 -> x0, blocking collectives: 17.7 us -> none  [sent_and_summed(): pieces = lax.all_to_all(in_blocks(x, dim, devices), axis, 0, 0, tiled=True)]
    dot_general x2 -> x0, matrix products: 7.79 us -> none  [the longest x1 6.22 us: on_device(): scores = jnp.dot(states, value_weight, preferred_element_type=jnp.float32)]
    all_gather x1 -> x0, waiting for transfers between devices: 6.77 us -> none  [over_pieces(): pieces = lax.all_gather(x, axis)]
    all_to_all x1 -> x0, starting transfers between devices: 4.2 us -> none  [sent_and_summed(): pieces = lax.all_to_all(in_blocks(x, dim, devices), axis, 0, 0, tiled=True)]
  transfers between devices with their start and end apart: 3 -> 0, of which waited for: 3 -> 0; matrix products, arithmetic and copies ran while one was open for 1% -> 0% of each run, Pallas kernels for 0% -> 0%
where the time goes in v1:
time: 60.5 us; the launch traced here: 60.3 us
  Pallas kernels  55 us (91%)
  local copies, waits for them, and re-layouts  4.68 us (8%)
  between operations  0.64 us (1%)
    pallas_call x1, Pallas kernels, on_device(): pl.pallas_call(functools.partial(kernel, rollouts), out_shape=(jax.ShapeD...  55 us
    unnamed x3, local copies, waits for them, and re-layouts  4.68 us

profile of v1, /device:TPU:1, one launch (start us, length us, event | category | flops | bytes accessed | tf_op | source)
XLA Modules:
  0.0 60.3 jit_solution(4014843074974909169)
XLA Ops:
  0.6 55.0 %shard_map.85 = (f32[1,1024]{1,0:T(1,128)}, f32[64,4096]{1,0:T(8,128)}, f32[1,64]{1,0:T(1,128)}) custom-call(bf16[1,1024,4096]{2,1,0:T(8,128)(2,1)} %hidden_hbm.1, bf16[64,4096]{1,0:T(8,128)(2,1)} %bitcast.5, f32[1,64]{1,0:T(1,128)} %bitcast.6, f32[1,1024]{1,0:T(1,128)} %returns_hbm.1, s32[1,1024]{1,0:T(1,128)} %bins_hbm.1, s32[1,1024]{1,0:T(1,128)} %mask_hbm.1), custom_call_target="tpu_custom_call" | custom-call | tf_op jit(solution)/shard_map/pallas_call | solution.py:316
  55.6 1.3 %copy.12 = f32[1,1024]{1,0:T(1,128)} copy(f32[1,1024]{1,0:T(1,128)} %get-tuple-element.12) | data formatting | bytes 8192
  56.9 2.3 %copy.13 = f32[4096,64]{0,1:T(8,128)} copy(f32[4096,64]{0,1:T(8,128)} %bitcast.4) | data formatting | bytes 2097152
  59.2 1.1 %copy.14 = f32[64]{0:T(128)} copy(f32[64]{0:T(128)} %bitcast.7) | data formatting | bytes 512

commit v2 on v1

v2 whole, which is shorter than its diff:
```python
import functools

import jax
import jax.numpy as jnp
from jax import lax
from jax.experimental import pallas as pl
from jax.experimental.pallas import tpu as pltpu
from jax.sharding import Mesh
from jax.sharding import PartitionSpec as P

NX, NZ, NY, NC = 4, 8, 4, 2
MESH = pl.DeviceIdType.MESH
HIGHEST = lax.Precision.HIGHEST
TOKENS, D, NB = 1024, 4096, 64
PIECES = 2
ROWS = TOKENS // PIECES
BLOCK = 512
HALF = D // 2
QUARTER = 256
PAIRS = ((2, 1), (3, 0))


def ring(k, n):
    return min(k, n - k)


LINE = sorted(((k, c) for k in range(NZ) for c in range(NC) if k or c), key=lambda p: -ring(p[0], NZ))
PLANE = sorted(((i, j) for i in range(NX) for j in range(NY) if i or j), key=lambda p: -ring(p[0], NX) - ring(p[1], NY))


def dot(a, b, dims, precision=None):
    return lax.dot_general(a, b, (dims, ((), ())), precision=precision, preferred_element_type=jnp.float32)


def ordered_sum(parts):
    total = parts[0]
    for part in parts[1:]:
        total = total + part
    return total


def kernel(
    rollouts,
    hidden_hbm, weight_hbm, bias_hbm, returns_hbm, bins_hbm, mask_hbm,
    targets_ref, grad_ref, bias_grad_ref,
    hidden, weight, bias, returns, bins, mask,
    predicted, coefficient,
    stats_line, stats_plane, bias_line, bias_plane,
    parts, from_core, summed, got_first, kept, got_second, got_third,
    hidden_sem, in_sem, small_send, small_recv,
    core_send, core_recv, first_send, first_recv, second_send, second_recv, third_send, third_recv,
    back_second_send, back_second_recv, back_first_send, back_first_recv, back_core_send, back_core_recv,
):
    x, z, y, c = (lax.axis_index(name) for name in ("x", "z", "y", "c"))

    def at(x=x, z=z, y=y, c=c):
        return {"x": x, "z": z, "y": y, "c": c}

    def in_line(k, core):
        return at(z=lax.rem(z + k, NZ), c=lax.rem(c + core, NC))

    def in_plane(i, j):
        return at(x=lax.rem(x + i, NX), y=lax.rem(y + j, NY))

    loads = [
        pltpu.make_async_copy(src, dst, in_sem.at[i])
        for i, (src, dst) in enumerate(
            ((returns_hbm, returns), (bins_hbm, bins), (mask_hbm, mask), (bias_hbm, bias), (weight_hbm, weight))
        )
    ]
    pieces = [
        pltpu.make_async_copy(
            hidden_hbm.at[0, pl.ds(i * ROWS, ROWS)], hidden.at[pl.ds(i * ROWS, ROWS)], hidden_sem.at[i]
        )
        for i in range(PIECES)
    ]
    for load in loads[:3]:
        load.start()
    barrier = pltpu.get_barrier_semaphore()
    for near, far in zip(LINE, PLANE):
        pl.semaphore_signal(barrier, inc=1, device_id=in_line(*near), device_id_type=MESH)
        pl.semaphore_signal(barrier, inc=1, device_id=in_plane(*far), device_id_type=MESH)
    for load in (loads[4], *pieces, loads[3]):
        load.start()

    def copy(src, dst, send, recv, peer):
        return pltpu.make_async_remote_copy(
            src_ref=src, dst_ref=dst, send_sem=send, recv_sem=recv, device_id=peer, device_id_type=MESH
        )

    def send_all(buffer, slot, sem, peers):
        for peer in peers:
            copy(buffer.at[slot], buffer.at[slot], small_send.at[sem], small_recv.at[sem], peer).start()

    def wait_all(buffer, sems, sem):
        fifteen = buffer.at[pl.ds(0, 15)]
        pltpu.make_async_copy(fifteen, fifteen, sems.at[sem]).wait()

    def total_of(buffer):
        return ordered_sum([buffer[i] for i in range(16)])

    line_peers = [in_line(*p) for p in LINE]
    plane_peers = [in_plane(*p) for p in PLANE]
    my_line = z * NC + c
    my_plane = x * NY + y

    for load in loads[:3]:
        load.wait()
    ret = returns[...]
    valid = mask[...].astype(jnp.float32)
    twice = ((lax.broadcasted_iota(jnp.int32, (2 * NB, TOKENS), 0) & (NB - 1)) == bins[...]).astype(jnp.float32)
    row = lax.broadcasted_iota(jnp.int32, (8, TOKENS), 0)
    moments = jnp.where(row == 0, valid, jnp.where(row == 1, valid * ret, jnp.where(row == 2, valid * ret * ret, 0.0)))
    local = dot(moments, twice, ((1,), (1,)), HIGHEST)
    lane = lax.broadcasted_iota(jnp.int32, (1, 2 * NB), 1)
    stats_line[my_line, 0:1] = jnp.where(lane < NB, local[0:1], local[1:2])
    stats_line[my_line, 1:2] = local[2:3]

    pl.semaphore_wait(barrier, 30)
    send_all(stats_line, my_line, 0, line_peers)

    def score(i):
        pieces[i].wait()
        rows = pl.ds(i * ROWS, ROWS)
        scores = dot(weight[...], hidden[rows, :], ((1,), (1,)))
        match = lax.broadcasted_iota(jnp.int32, (NB, ROWS), 0) == bins[:, rows]
        predicted[:, rows] = jnp.sum(jnp.where(match, scores, 0.0), axis=0, keepdims=True)

    loads[4].wait()
    score(0)
    wait_all(stats_line, small_recv, 0)
    stats_plane[my_plane] = total_of(stats_line)
    send_all(stats_plane, my_plane, 1, plane_peers)
    score(1)
    loads[3].wait()
    wait_all(stats_line, small_send, 0)
    wait_all(stats_plane, small_recv, 1)
    total = total_of(stats_plane)

    counts = jnp.maximum(total[0:1, :NB], 1.0)
    sums = total[0:1, NB:]
    means = sums / counts
    second = total[1:2, :NB] - sums * means
    spread = jnp.sqrt(second / counts + 0.1)
    table_row = lax.broadcasted_iota(jnp.int32, (8, NB), 0)
    table = jnp.where(
        table_row == 0, means, jnp.where(table_row == 1, spread, jnp.where(table_row == 2, bias[...], 0.0))
    )
    chosen = (lax.broadcasted_iota(jnp.int32, (NB, TOKENS), 0) == bins[...]).astype(jnp.float32)
    own = dot(table, chosen, ((1,), (0,)), HIGHEST)
    targets = (returns[...] - own[0:1]) / own[1:2]
    targets_ref[...] = targets
    slope = mask[...].astype(jnp.float32) * jnp.clip(predicted[...] + own[2:3] - targets, -1.0, 1.0) / rollouts
    predicted[...] = slope
    coefficient[...] = (chosen * slope).astype(jnp.bfloat16)

    mine = pl.ds(pl.multiple_of(c * 32, 32), 32)
    others = pl.ds(pl.multiple_of((1 - c) * 32, 32), 32)
    first_at, second_at = (x, y), (y, x)

    def first_peer(half, k):
        return at(x=lax.rem(x + k, NX)) if half == 0 else at(y=lax.rem(y + k, NY))

    def second_peer(half, k):
        return at(y=lax.rem(y + k, NY)) if half == 0 else at(x=lax.rem(x + k, NX))

    def parity(group):
        return lax.rem(z + 1 + group, 2)

    def core_copy(s):
        return copy(parts.at[s, others], from_core.at[s], core_send.at[s], core_recv.at[s], at(c=1 - c))

    def first_copy(group, half, k):
        pair = next(i for i, ks in enumerate(PAIRS) if k in ks)
        spot = (PAIRS[pair].index(k) * 2 + half) * QUARTER
        return copy(
            summed.at[group * 2 + pair, :, pl.ds(spot, QUARTER)], got_first.at[group, half, k - 1],
            first_send.at[group, half, k - 1], first_recv.at[group, half, k - 1], first_peer(half, k),
        )

    for group in range(2):
        for pair, ks in enumerate(PAIRS):
            s = group * 2 + pair
            blocks = [
                hidden[:, pl.ds(
                    pl.multiple_of(
                        half * HALF + lax.rem(first_at[half] + k, 4) * BLOCK + parity(group) * QUARTER, QUARTER
                    ), QUARTER
                )]
                for k in ks for half in range(2)
            ]
            parts[s] = dot(coefficient[...], jnp.concatenate(blocks, axis=1), ((1,), (0,)))
            core_copy(s).start()
    for group in range(2):
        for pair, ks in enumerate(PAIRS):
            s = group * 2 + pair
            core_copy(s).wait_recv()
            summed[s] = parts[s, mine] + from_core[s]
            for k in ks:
                if k:
                    for half in range(2):
                        first_copy(group, half, k).start()

    chosen = (lax.broadcasted_iota(jnp.int32, (2 * NB, TOKENS), 0) == bins[...]).astype(jnp.float32)
    slopes = jnp.where(row == 0, predicted[...], 0.0)
    bias_line[my_line] = dot(slopes, chosen, ((1,), (1,)), HIGHEST)[0:1]
    send_all(bias_line, my_line, 2, line_peers)
    wait_all(stats_plane, small_send, 1)

    def second_copy(half, k):
        there = lax.rem(z + k, NZ)
        return copy(
            kept.at[(k + 1) % 2, half, pl.ds(pl.multiple_of(there // 2 * 8, 8), 8)], got_second.at[half, k - 1],
            second_send.at[half, k - 1], second_recv.at[half, k - 1], at(z=there),
        )

    for group, distances in enumerate(((3, 5, 1, 7), (4, 2, 6))):
        for half in range(2):
            for k in (1, 3, 2):
                first_copy(group, half, k).wait_recv()
            own_part = summed[group * 2 + 1, :, (2 + half) * QUARTER : (3 + half) * QUARTER]
            kept[group, half] = ordered_sum([own_part] + [got_first[group, half, i] for i in range(3)])
            for k in distances:
                second_copy(half, k).start()
    for s in range(4):
        core_copy(s).wait_send()

    wait_all(bias_line, small_recv, 2)
    bias_plane[my_plane] = total_of(bias_line)
    send_all(bias_plane, my_plane, 3, plane_peers)
    wait_all(bias_line, small_send, 2)

    def third_copy(half, k):
        slot = got_third.at[half, second_at[half]]
        return copy(slot, slot, third_send.at[half, k - 1], third_recv.at[half, k - 1], second_peer(half, k))

    for half in range(2):
        for k in (1, 7, 2, 6, 3, 5, 4):
            second_copy(half, k).wait_recv()
        own_part = kept[1, half, pl.ds(pl.multiple_of(z // 2 * 8, 8), 8)]
        got_third[half, second_at[half]] = ordered_sum([own_part] + [got_second[half, i] for i in range(7)])
        for k in (2, 1, 3):
            third_copy(half, k).start()
    for group in range(2):
        for half in range(2):
            for k in (1, 2, 3):
                first_copy(group, half, k).wait_send()

    def place(half, z):
        return grad_ref.at[
            pl.ds(pl.multiple_of(c * 32 + z // 2 * 8, 8), 8),
            pl.ds(pl.multiple_of(half * HALF + first_at[half] * BLOCK + lax.rem(z, 2) * QUARTER, QUARTER), QUARTER),
        ]

    def back_second(half, k):
        spot = place(half, z)
        return copy(
            spot, spot, back_second_send.at[half, k - 1], back_second_recv.at[half, k - 1], at(z=lax.rem(z + k, NZ))
        )

    def block_of(half, owner):
        return grad_ref.at[mine, pl.ds(pl.multiple_of(half * HALF + owner * BLOCK, BLOCK), BLOCK)]

    def back_first_part(half, k, distance):
        spot = place(half, lax.rem(z + NZ - distance, NZ))
        return copy(spot, spot, back_first_send.at[half, k - 1], back_first_recv.at[half, k - 1], first_peer(half, k))

    def back_first(half, k):
        spot = block_of(half, first_at[half])
        return copy(spot, spot, back_first_send.at[half, k - 1], back_first_recv.at[half, k - 1], first_peer(half, k))

    def back_core(half, k):
        spot = block_of(half, lax.rem(first_at[half] + 4 - k, 4))
        return copy(spot, spot, back_core_send.at[half, k], back_core_recv.at[half, k], at(c=1 - c))

    for half in range(2):
        for k in (1, 3, 2):
            third_copy(half, k).wait_recv()
        place(half, z)[...] = ordered_sum([got_third[half, i] for i in range(4)])
        for k in (4, 3, 5, 2, 6, 1, 7):
            back_second(half, k).start()
    for half in range(2):
        for k in range(1, NZ):
            second_copy(half, k).wait_send()
        for k in (1, 2, 3):
            third_copy(half, k).wait_send()
    for distance in (0, 1, 7, 2, 6, 3, 5, 4):
        for half in range(2):
            if distance:
                back_second(half, distance).wait_recv()
            for k in (2, 1, 3):
                back_first_part(half, k, distance).start()
    for half in range(2):
        back_core(half, 0).start()

    wait_all(bias_plane, small_recv, 3)
    bias_grad_ref[...] = total_of(bias_plane)[0:1, :NB]
    wait_all(bias_plane, small_send, 3)
    for half in range(2):
        for k in range(1, NZ):
            back_second(half, k).wait_send()

    for k in (1, 3, 2):
        for half in range(2):
            back_first(half, k).wait_recv()
            back_core(half, k).start()
    for half in range(2):
        for k in (1, 2, 3):
            back_first(half, k).wait_send()
    for k in (0, 1, 3, 2):
        for half in range(2):
            back_core(half, k).wait()


def write_out(targets, grad, bias_grad, targets_hbm, grad_hbm, bias_grad_hbm, sem):
    copies = [
        pltpu.make_async_copy(src, dst, sem.at[i])
        for i, (src, dst) in enumerate(
            ((grad, grad_hbm), (targets, targets_hbm), (bias_grad, bias_grad_hbm))
        )
    ]
    for copy in copies:
        copy.start()
    for copy in copies:
        copy.wait()


def on_device(hidden, value_weight, value_bias, returns, task_bins, loss_mask):
    rollouts = hidden.shape[0] * lax.axis_size(("x", "z"))
    f32 = jnp.float32
    dma = pltpu.SemaphoreType.DMA
    any_space = pl.BlockSpec(memory_space=pl.ANY)
    vmem = pl.BlockSpec(memory_space=pltpu.VMEM)
    pair, single = pltpu.VMEM((16, 2, 128), f32), pltpu.VMEM((16, 1, 128), f32)
    shapes = ((1, TOKENS), (NB, D), (1, NB))
    results = pl.pallas_call(
        functools.partial(kernel, rollouts),
        out_shape=tuple(pltpu.VMEM(shape, f32) for shape in shapes),
        in_specs=[any_space] * 6,
        out_specs=(vmem, vmem, vmem),
        scratch_shapes=[
            pltpu.VMEM((TOKENS, D), jnp.bfloat16),
            pltpu.VMEM((NB, D), jnp.bfloat16),
            pltpu.VMEM((1, NB), f32),
            pltpu.VMEM((1, TOKENS), f32),
            pltpu.VMEM((1, TOKENS), jnp.int32),
            pltpu.VMEM((1, TOKENS), jnp.int32),
            pltpu.VMEM((1, TOKENS), f32),
            pltpu.VMEM((NB, TOKENS), jnp.bfloat16),
            pair, pair, single, single,
            pltpu.VMEM((4, NB, 4 * QUARTER), f32),
            pltpu.VMEM((4, 32, 4 * QUARTER), f32),
            pltpu.VMEM((4, 32, 4 * QUARTER), f32),
            pltpu.VMEM((2, 2, 3, 32, QUARTER), f32),
            pltpu.VMEM((2, 2, 32, QUARTER), f32),
            pltpu.VMEM((2, 7, 8, QUARTER), f32),
            pltpu.VMEM((2, 4, 8, QUARTER), f32),
            dma((PIECES,)), dma((5,)), dma((4,)), dma((4,)),
            dma((4,)), dma((4,)), dma((2, 2, 3)), dma((2, 2, 3)), dma((2, 7)), dma((2, 7)), dma((2, 3)), dma((2, 3)),
            dma((2, 7)), dma((2, 7)), dma((2, 3)), dma((2, 3)), dma((2, 4)), dma((2, 4)),
        ],
        compiler_params=pltpu.CompilerParams(
            collective_id=0, has_side_effects=True, vmem_limit_bytes=60 * 1024 * 1024
        ),
    )(hidden, value_weight.T, value_bias.reshape(1, NB), returns, task_bins, loss_mask)
    targets, grad, bias_grad = pl.pallas_call(
        write_out,
        out_shape=tuple(jax.ShapeDtypeStruct(shape, f32) for shape in shapes),
        in_specs=[vmem] * 3,
        out_specs=(any_space,) * 3,
        scratch_shapes=[dma((3,))],
    )(*(pltpu.with_memory_space_constraint(r, pltpu.VMEM) for r in results))
    return targets, grad.T, bias_grad.reshape(NB)


def solution(mesh):
    torus = Mesh(mesh.devices.reshape(NX, NZ, NY, NC), ("x", "z", "y", "c"))
    dp, seq = ("x", "z"), ("y", "c")
    return jax.shard_map(
        on_device,
        mesh=torus,
        in_specs=(P(dp, seq, None), P(), P(), P(dp, seq), P(dp, seq), P(dp, seq)),
        out_specs=(P(dp, seq), P(), P()),
        check_vma=False,
    )
```

time: 60.5 us -> 49.6 us (0.82)
  Pallas kernels: 55 us -> 48.8 us
  local copies, waits for them, and re-layouts: 4.68 us -> 0 us
    pallas_call x1 -> x2, Pallas kernels: 55 us -> 48.8 us  [the longest x1 47.8 us: on_device(): pl.pallas_call(functools.partial(kernel, rollouts), out_shape=tuple((pltp...]
    unnamed x3 -> x0, local copies, waits for them, and re-layouts: 4.68 us -> none
where the time goes in v2:
time: 49.6 us; the launch traced here: 49.5 us
  Pallas kernels  48.8 us (98%)
  between operations  0.64 us (1%)
    pallas_call x1, Pallas kernels, on_device(): pl.pallas_call(functools.partial(kernel, rollouts), out_shape=tuple((pltp...  47.8 us
    pallas_call x1, Pallas kernels, on_device(): pl.pallas_call(write_out, out_shape=tuple((jax.ShapeDtypeStruct(shape, f3...  1 us

profile of v2, /device:TPU:1, one launch (start us, length us, event | category | flops | bytes accessed | tf_op | source)
XLA Modules:
  0.0 49.5 jit_solution(12745313710204831436)
XLA Ops:
  0.6 47.8 %shard_map.85 = (f32[1,1024]{1,0:T(1,128)S(1)}, f32[64,4096]{1,0:T(8,128)S(1)}, f32[1,64]{1,0:T(1,128)S(1)}) custom-call(bf16[1,1024,4096]{2,1,0:T(8,128)(2,1)} %hidden_hbm.1, bf16[64,4096]{1,0:T(8,128)(2,1)} %bitcast.4, f32[1,64]{1,0:T(1,128)} %bitcast.5, f32[1,1024]{1,0:T(1,128)} %returns_hbm.1, s32[1,1024]{1,0:T(1,128)} %bins_hbm.1, s32[1,1024]{1,0:T(1,128)} %mask_hbm.1), custom_call_target="tpu_custom_call" | custom-call | tf_op jit(solution)/shard_map/pallas_call | solution.py:336
  48.5 1.0 %shard_map.86 = (f32[1,1024]{1,0:T(1,128)}, f32[64,4096]{1,0:T(8,128)}, f32[1,64]{1,0:T(1,128)}) custom-call(f32[1,1024]{1,0:T(1,128)S(1)} %get-tuple-element.9.targets, f32[64,4096]{1,0:T(8,128)S(1)} %get-tuple-element.10.grad, f32[1,64]{1,0:T(1,128)S(1)} %get-tuple-element.11.bias_grad), custom_call_target="tpu_custom_call" | custom-call | tf_op jit(solution)/shard_map/pallas_call | solution.py:366
